TPU v7x, 128 devices: a whole 4x4x4 slice. The times are simulated.
128 devices in a mesh: gx: 16 (over z, x), gy: 8 (over y, core).
Axes of the slice: x: 4, y: 4, z: 4, core: 2. Of those that a mesh axis runs over, the one named last changes fastest.
Arguments:
- density: float32 [1024, 256, 128], P('gx', 'gy'), may hold values from -6 to 6
- slowness: float32 [1024, 256, 128], P('gx', 'gy'), may hold values from -6 to 6
- pressure_obs: float32 [1024, 256, 128], P('gx', 'gy'), may hold values from -6 to 6
- time_obs: float32 [1024, 256, 128], P('gx', 'gy'), may hold values from -6 to 6
- zone_map: int32 [1024, 256, 128], P('gx', 'gy'), may hold values from 0 to 7
- zone_low: float32 [8], replicated, may hold values from -2.5 to -0.5
- zone_high: float32 [8], replicated, may hold values from 0.5 to 2.5
Outputs:
- density_out: float32 [1024, 256, 128], P('gx', 'gy')
- slowness_out: float32 [1024, 256, 128], P('gx', 'gy')
- objective: float32 [3], replicated
All inputs are finite; a program needn't handle non-finite values.
Results may differ from a plain program's by a relative error of at most 0.00013.
Values sent between devices are 32-bit elements; how exact they have to be, the bound alone decides.
A program may use at most 128 MiB of HBM per device.

v0:
```python
import math
import jax
import jax.numpy as jnp
from jax import lax
from jax.sharding import Mesh
from jax.sharding import PartitionSpec as P

ITERS = 3
GX_GY = ("gx_0", "gx_1", "gy_0", "gy_1")
GX = ("gx_0", "gx_1")
GY = ("gy_0", "gy_1")
BETA = 1.0
ETA = 0.5
EPSILON = 1e-06


def over_axes(value, axes):
    for axis in axes:
        value = lax.psum(value, axis)
    return value


def laid_out(tiles, dim):
    tiles = jnp.moveaxis(tiles, 0, dim)
    dims = tiles.shape
    return tiles.reshape(*dims[:dim], dims[dim] * dims[dim + 1], *dims[dim + 2 :])


def copy_for_each(value, axis):
    copies = jnp.broadcast_to(value, (lax.axis_size(axis), *value.shape))
    return lax.all_to_all(copies, axis, split_axis=0, concat_axis=0, tiled=True)


def collect(value, axis, dim):
    return laid_out(copy_for_each(value, axis), dim)


def with_halo(value, sides, width):
    for axis, dim in sides:
        size, length = (lax.axis_size(axis), value.shape[dim])
        up = [(i, (i + 1) % size) for i in range(size - 1)]
        down = [(j, i) for i, j in up]
        last = lax.slice_in_dim(value, length - width, length, axis=dim)
        initial = lax.slice_in_dim(value, 0, width, axis=dim)
        before = lax.ppermute(last, axis, up)
        after = lax.ppermute(initial, axis, down)
        value = jnp.concatenate([before, value, after], axis=dim)
    return value


def cross_product(first_vec, second_vec):
    return (
        first_vec[1] * second_vec[2] - first_vec[2] * second_vec[1],
        first_vec[2] * second_vec[0] - first_vec[0] * second_vec[2],
        first_vec[0] * second_vec[1] - first_vec[1] * second_vec[0],
    )


def depth_slope(inner):
    padded = jnp.pad(inner, [(0, 0)] * (inner.ndim - 1) + [(1, 1)])
    return (padded[..., 2:] - padded[..., :-2]) * 0.5


def depth_adjoint(values):
    padded = jnp.pad(values, [(0, 0)] * (values.ndim - 1) + [(1, 1)])
    return (padded[..., :-2] - padded[..., 2:]) * 0.5


def block_slopes(padded):
    along_x = (padded[:, 2:, 1:-1] - padded[:, :-2, 1:-1]) * 0.5
    along_y = (padded[:, 1:-1, 2:] - padded[:, 1:-1, :-2]) * 0.5
    along_z = depth_slope(padded[:, 1:-1, 1:-1])
    return (along_x, along_y, along_z)


def triangle(length, upward):
    first = jnp.arange(length)[:, None]
    second = jnp.arange(length)[None, :]
    if upward:
        return (first <= second).astype(jnp.float32)
    return (first >= second).astype(jnp.float32)


def depth_prefix(values, upward):
    table = triangle(values.shape[-1], upward)
    return jnp.einsum("xyj,jk->xyk", values, table, precision=lax.Precision.HIGHEST)


def rows_prefix(values, upward):
    table = triangle(values.shape[0], not upward)
    return jnp.einsum("ij,jyz->iyz", table, values, precision=lax.Precision.HIGHEST)


def global_sums(values):
    return (over_axes(values[0], GX_GY), over_axes(values[1], GX_GY), over_axes(values[2], GX_GY))


def local(density, slowness, pressure_obs, time_obs, zone_map, zone_low, zone_high):
    size_x, size_y, depth = density.shape
    parts_x = lax.axis_size(GX)
    parts_y = lax.axis_size(GY)
    total_x = size_x * parts_x
    total_y = size_y * parts_y
    cells = float(total_x * total_y * depth)
    zscale = 1.0 / math.sqrt(depth)
    xscale = 1.0 / math.sqrt(total_x)
    lower_bound = jnp.zeros(density.shape, jnp.float32)
    upper_bound = jnp.zeros(density.shape, jnp.float32)
    for zone_index in range(zone_low.shape[0]):
        hit = zone_map == zone_index
        lower_bound = jnp.where(hit, zone_low[zone_index], lower_bound)
        upper_bound = jnp.where(hit, zone_high[zone_index], upper_bound)
    my_x = lax.axis_index(GX)
    my_y = lax.axis_index(GY)
    anchor_x = my_x * size_x
    anchor_y = my_y * size_y
    shard_ids = jnp.arange(parts_x)
    own_weight = (shard_ids == my_x).astype(jnp.float32)
    later_weight = (shard_ids > my_x).astype(jnp.float32)
    earlier_table = (shard_ids[:, None] > shard_ids[None, :]).astype(jnp.float32)
    observed_totals = collect(jnp.sum(time_obs, 0)[None], GX, 0)
    observed_later = jnp.einsum(
        "k,kyz->yz", later_weight, observed_totals, precision=lax.Precision.HIGHEST
    )
    density_now = density
    slowness_now = slowness
    history = []
    for iteration in range(ITERS):
        fields = jnp.stack((density_now, slowness_now))
        padded = with_halo(fields, ((GX, 1), (GY, 2)), 2)
        along_x, along_y, along_z = block_slopes(padded)
        first_vec = (along_x[0], along_y[0], along_z[0])
        second_vec = (along_x[1], along_y[1], along_z[1])
        crossed_wide = cross_product(first_vec, second_vec)
        toward_density = cross_product(second_vec, crossed_wide)
        toward_slowness = cross_product(crossed_wide, first_vec)
        rows_x = anchor_x - 1 + jnp.arange(size_x + 2)
        rows_y = anchor_y - 1 + jnp.arange(size_y + 2)
        inside_x = (rows_x >= 0) & (rows_x < total_x)
        inside_y = (rows_y >= 0) & (rows_y < total_y)
        inside = (inside_x[:, None] & inside_y[None, :]).astype(jnp.float32)[:, :, None]
        side_x = jnp.stack((toward_density[0], toward_slowness[0])) * inside
        side_y = jnp.stack((toward_density[1], toward_slowness[1])) * inside
        back_x = (side_x[:, :-2, 1:-1] - side_x[:, 2:, 1:-1]) * 0.5
        back_y = (side_y[:, 1:-1, :-2] - side_y[:, 1:-1, 2:]) * 0.5
        depth_parts = jnp.stack((toward_density[2], toward_slowness[2]))[:, 1:-1, 1:-1]
        back_z = depth_adjoint(depth_parts)
        crossed = tuple((member[1:-1, 1:-1] for member in crossed_wide))
        cross_term = back_x + back_y + back_z
        pressure_miss = depth_prefix(density_now, True) * zscale - pressure_obs
        running = rows_prefix(slowness_now, True)
        stacked = jnp.stack((running[-1], jnp.sum(running, 0)))[None]
        gathered = collect(stacked, GX, 0)
        befores = jnp.einsum(
            "kj,jyz->kyz", earlier_table, gathered[:, 0], precision=lax.Precision.HIGHEST
        )
        before = jnp.einsum("k,kyz->yz", own_weight, befores, precision=lax.Precision.HIGHEST)
        shard_sums = gathered[:, 1] + float(size_x) * befores
        after_early = (
            jnp.einsum("k,kyz->yz", later_weight, shard_sums, precision=lax.Precision.HIGHEST)
            * xscale
            - observed_later
        )
        time_miss = (running + before[None]) * xscale - time_obs
        backward = rows_prefix(time_miss, False)
        column_back = depth_prefix(pressure_miss, False)
        grad_density = column_back * zscale + BETA * cross_term[0]
        grad_slowness = (backward + after_early[None]) * xscale + BETA * cross_term[1]
        crossed_sq = (
            jnp.sum(crossed[0] * crossed[0])
            + jnp.sum(crossed[1] * crossed[1])
            + jnp.sum(crossed[2] * crossed[2])
        )
        local_objective = (
            0.5
            * (
                jnp.sum(pressure_miss * pressure_miss)
                + jnp.sum(time_miss * time_miss)
                + BETA * crossed_sq
            )
            / cells
        )
        local_density = jnp.sum(grad_density * grad_density)
        local_slowness = jnp.sum(grad_slowness * grad_slowness)
        objective_now, norm_density, norm_slowness = global_sums(
            (local_objective, local_density, local_slowness)
        )
        history.append(objective_now)
        moved = density_now - ETA * grad_density * lax.rsqrt(norm_density / cells + EPSILON)
        density_now = jnp.minimum(jnp.maximum(moved, lower_bound), upper_bound)
        slowness_now = slowness_now - ETA * grad_slowness * lax.rsqrt(
            norm_slowness / cells + EPSILON
        )
    objective = jnp.stack(history)
    return (density_now, slowness_now, objective)


def solution(mesh):
    torus = Mesh(mesh.devices.reshape(4, 4, 4, 2), ("gx_0", "gx_1", "gy_0", "gy_1"))
    in_specs = (
        P(GX, GY, None),
        P(GX, GY, None),
        P(GX, GY, None),
        P(GX, GY, None),
        P(GX, GY, None),
        P(),
        P(),
    )
    out_specs = (P(GX, GY, None), P(GX, GY, None), P())
    return jax.shard_map(local, mesh=torus, in_specs=in_specs, out_specs=out_specs, check_vma=False)
```

profile of v0, /device:TPU:1, one launch (start us, length us, event | category | flops | bytes accessed | tf_op | source)
XLA Modules:
  0.0 324.0 jit_solution(1561969263531289439)
XLA Ops:
  1.6 3.9 %collective-permute-start = (f32[2,2,32,128]{3,2,1,0:T(8,128)S(1)}, f32[2,2,32,128]{3,2,1,0:T(8,128)S(1)}, u32[]{:S(2)}, u32[]{:S(2)}) collective-permute-start(f32[2,2,32,128]{3,2,1,0:T(8,128)S(1)} %get-tuple-element.91), channel_id=1, source_target_pairs={{0,8},{8,16},{16,24},{24,32},{32,40},{40,48},{48,56},{56,64},{64,7... | collective-permute-start | bytes 196616 | tf_op jit(solution)/shard_map/ppermute | solution.py:45
  10.1 8.5 %all-to-all-start = ((f32[16,1,2,32,128]{4,3,2,1,0:T(8,128)}), f32[16,1,2,32,128]{4,3,2,1,0:T(8,128)}, u32[]{:S(2)}, u32[]{:S(2)}) async-start(f32[16,1,2,32,128]{4,3,2,1,0:T(8,128)} %broadcast_in_dim.119), calls=%async_computation | async-start | bytes 1048576 | tf_op jit(solution)/shard_map/all_to_all | solution.py:31
  18.7 3.4 %multiply_reduce_fusion.5 = (f32[]{:T(128)}, f32[64,32,128]{2,0,1:T(8,128)}) fusion(f32[64,32,128]{2,1,0:T(8,128)S(1)} %copy-done.6, f32[64,32,128]{2,1,0:T(8,128)S(1)} %copy-done.1), kind=kOutput, calls=%fused_computation.182 | convolution fusion | flops 403718144 | bytes 3145732 | tf_op jit(solution)/shard_map/xyj,jk->xyk/dot_general | solution.py:86
  22.1 2.2 broadcast_compare_fusion
  24.5 4.6 %collective-permute-start.3 = (f32[2,68,2,128]{3,2,1,0:T(2,128)S(1)}, f32[2,68,2,128]{3,2,1,0:T(2,128)S(1)}, u32[]{:S(2)}, u32[]{:S(2)}) collective-permute-start(f32[2,68,2,128]{3,2,1,0:T(2,128)S(1)} %get-tuple-element.85), channel_id=1, source_target_pairs={{0,1},{1,2},{2,3},{3,4},{4,5},{5,6},{6,7},{8,9},{9,10},{10,11},{11... | collective-permute-start | bytes 417800 | tf_op jit(solution)/shard_map/ppermute | solution.py:45
  29.1 2.1 collective-permute-start.2
  32.6 2.9 collective-permute-done.2
  36.2 1.5 fusion.2
  37.7 1.6 fusion.15
  39.4 1.5 multiply_subtract_fusion.24
  41.4 1.8 multiply_subtract_fusion.19
  45.6 2.2 fusion.23
  51.5 4.1 %multiply_reduce_fusion.11 = (f32[]{:T(128)}, f32[64,32,128]{2,1,0:T(8,128)}) fusion(f32[2,64,32,128]{3,2,1,0:T(8,128)} %fusion.23, f32[64,32,128]{2,0,1:T(8,128)S(1)} %copy-done.24), kind=kOutput, calls=%fused_computation.196 | convolution fusion | flops 403718144 | bytes 3145732 | tf_op jit(solution)/shard_map/xyj,jk->xyk/dot_general | solution.py:86
  57.8 3.9 %multiply_reduce_fusion.4 = (f32[]{:T(128)}, f32[64,32,128]{2,1,0:T(8,128)}, f32[32,128]{1,0:T(8,128)S(1)}) fusion(f32[64,32,128]{2,1,0:T(8,128)} %param.10, f32[32,128]{1,0:T(8,128)S(1)} %bitcast.239, f32[64,32,128]{2,0,1:T(8,128)} %copy-done.19), kind=kLoop, calls=%fused_computation.181 | loop fusion | flops 1568767 | bytes 3178500 | tf_op jit(solution)/shard_map/reduce_sum | solution.py:178
  62.5 7.2 %all-to-all-start.1 = ((f32[16,1,32,128]{3,2,1,0:T(8,128)}), f32[16,1,32,128]{3,2,1,0:T(8,128)}, u32[]{:S(2)}, u32[]{:S(2)}) async-start(f32[16,1,32,128]{3,2,1,0:T(8,128)} %broadcast_in_dim.120), calls=%async_computation.1 | async-start | bytes 524288 | tf_op jit(solution)/shard_map/all_to_all | solution.py:31
  69.6 3.4 %fusion.59 = f32[64,32,128]{2,0,1:T(8,128)} fusion(f32[64,32,128]{2,1,0:T(8,128)} %get-tuple-element.40), kind=kOutput, calls=%fused_computation.168 | convolution fusion | flops 201330688 | bytes 2097152 | tf_op jit(solution)/shard_map/ij,jyz->iyz/dot_general | solution.py:91
  75.4 1.7 all-to-all-done.1
  78.5 2.5 multiply_reduce_fusion.10
  81.0 7.5 %all-reduce.14 = (f32[]{:T(128)}, f32[]{:T(128)}) all-reduce(f32[]{:T(128)} %get-tuple-element.124, f32[]{:T(128)} %multiply_reduce_fusion.10), channel_id=1, replica_groups=mesh['gx_0'=4,'gx_1'=4,'gy_0'=4,'gy_1'=2] {'gx_0'}, use_global_device_ids=true, to_apply=%region_1.2 | all-reduce | flops 2 | bytes 16 | tf_op jit(solution)/shard_map/psum | solution.py:19
  88.6 9.2 %all-reduce.11 = (f32[]{:T(128)}, f32[]{:T(128)}) all-reduce(f32[]{:T(128)} %get-tuple-element.28, f32[]{:T(128)} %get-tuple-element.29), channel_id=1, replica_groups=mesh['gx_0'=4,'gx_1'=4,'gy_0'=4,'gy_1'=2] {'gx_1'}, use_global_device_ids=true, to_apply=%region_2.3 | all-reduce | flops 2 | bytes 16 | tf_op jit(solution)/shard_map/psum | solution.py:19
  97.8 7.7 %all-reduce.8 = (f32[]{:T(128)}, f32[]{:T(128)}) all-reduce(f32[]{:T(128)} %get-tuple-element.19, f32[]{:T(128)} %get-tuple-element.20), channel_id=1, replica_groups=mesh['gx_0'=4,'gx_1'=4,'gy_0'=4,'gy_1'=2] {'gy_0'}, use_global_device_ids=true, to_apply=%region_3.4 | all-reduce | flops 2 | bytes 16 | tf_op jit(solution)/shard_map/psum | solution.py:19
  105.6 9.5 %all-reduce.17 = (f32[]{:T(128)}, f32[]{:T(128)}) all-reduce(f32[]{:T(128)} %get-tuple-element.10, f32[]{:T(128)} %get-tuple-element.11), channel_id=1, replica_groups=mesh['gx_0'=4,'gx_1'=4,'gy_0'=4,'gy_1'=2] {'gy_1'}, use_global_device_ids=true, to_apply=%region_4.5 | all-reduce | flops 2 | bytes 16 | tf_op jit(solution)/shard_map/psum | solution.py:19
  116.4 2.2 multiply_subtract_fusion.29
  118.7 14.6 %maximum_minimum_fusion.2 = (f32[64,32,128]{2,1,0:T(8,128)S(1)}, f32[64,32,128]{2,1,0:T(8,128)}, f32[64,32,128]{2,1,0:T(8,128)}) fusion(f32[64,32,128]{2,1,0:T(8,128)} %param.7, f32[64,32,128]{2,1,0:T(8,128)} %get-tuple-element.125, f32[]{:T(128)S(6)} %mul.590, pred[64,32,128]{2,1,0:T(8,128)(4,1)} %get-tuple-element.99, ...), kind=kLoop, calls=%fused_computation.194 | loop fusion | flops 5242880 | bytes 7340100 | tf_op jit(solution)/shard_map/min | solution.py:190
  133.3 1.6 collective-permute-start.4
  136.2 2.2 multiply_reduce_fusion.3
  138.4 1.5 collective-permute-done.5
  140.0 3.9 %collective-permute-start.7 = (f32[2,68,2,128]{3,2,1,0:T(2,128)S(1)}, f32[2,68,2,128]{3,2,1,0:T(2,128)S(1)}, u32[]{:S(2)}, u32[]{:S(2)}) collective-permute-start(f32[2,68,2,128]{3,2,1,0:T(2,128)S(1)} %get-tuple-element.83), channel_id=1, source_target_pairs={{0,1},{1,2},{2,3},{3,4},{4,5},{5,6},{6,7},{8,9},{9,10},{10,11},{11... | collective-permute-start | bytes 417800 | tf_op jit(solution)/shard_map/ppermute | solution.py:45
  143.9 1.9 collective-permute-start.6
  149.1 7.0 %all-to-all-start.2 = ((f32[16,1,2,32,128]{4,3,2,1,0:T(8,128)}), f32[16,1,2,32,128]{4,3,2,1,0:T(8,128)}, u32[]{:S(2)}, u32[]{:S(2)}) async-start(f32[16,1,2,32,128]{4,3,2,1,0:T(8,128)} %broadcast_in_dim.121), calls=%async_computation.2 | async-start | bytes 1048576 | tf_op jit(solution)/shard_map/all_to_all | solution.py:31
  157.0 1.5 fusion.4
  158.4 1.6 fusion.12
  160.1 1.5 multiply_subtract_fusion.15
  162.7 1.8 multiply_subtract_fusion.10
  166.9 2.2 fusion.20
  171.2 2.2 fusion.35
  174.0 3.9 %multiply_reduce_fusion.9 = (f32[]{:T(128)}, f32[64,32,128]{2,1,0:T(8,128)}) fusion(f32[2,64,32,128]{3,2,1,0:T(8,128)} %fusion.20, f32[64,32,128]{2,1,0:T(8,128)} %get-tuple-element.139), kind=kOutput, calls=%fused_computation.190 | convolution fusion | flops 403718144 | bytes 3145732 | tf_op jit(solution)/shard_map/xyj,jk->xyk/dot_general | solution.py:86
  177.8 1.4 copy.135
  184.0 9.4 %all-reduce.13 = (f32[]{:T(128)}, f32[]{:T(128)}) all-reduce(f32[]{:T(128)} %get-tuple-element.128, f32[]{:T(128)} %multiply_reduce_fusion.8), channel_id=1, replica_groups=mesh['gx_0'=4,'gx_1'=4,'gy_0'=4,'gy_1'=2] {'gx_0'}, use_global_device_ids=true, to_apply=%region_13.14 | all-reduce | flops 2 | bytes 16 | tf_op jit(solution)/shard_map/psum | solution.py:19
  193.3 9.0 %all-reduce.10 = (f32[]{:T(128)}, f32[]{:T(128)}) all-reduce(f32[]{:T(128)} %get-tuple-element.26, f32[]{:T(128)} %get-tuple-element.27), channel_id=1, replica_groups=mesh['gx_0'=4,'gx_1'=4,'gy_0'=4,'gy_1'=2] {'gx_1'}, use_global_device_ids=true, to_apply=%region_14.15 | all-reduce | flops 2 | bytes 16 | tf_op jit(solution)/shard_map/psum | solution.py:19
  202.3 7.1 %all-reduce.7 = (f32[]{:T(128)}, f32[]{:T(128)}) all-reduce(f32[]{:T(128)} %get-tuple-element.17, f32[]{:T(128)} %get-tuple-element.18), channel_id=1, replica_groups=mesh['gx_0'=4,'gx_1'=4,'gy_0'=4,'gy_1'=2] {'gy_0'}, use_global_device_ids=true, to_apply=%region_15.16 | all-reduce | flops 2 | bytes 16 | tf_op jit(solution)/shard_map/psum | solution.py:19
  209.4 10.8 %all-reduce.16 = (f32[]{:T(128)}, f32[]{:T(128)}) all-reduce(f32[]{:T(128)} %get-tuple-element.8, f32[]{:T(128)} %get-tuple-element.9), channel_id=1, replica_groups=mesh['gx_0'=4,'gx_1'=4,'gy_0'=4,'gy_1'=2] {'gy_1'}, use_global_device_ids=true, to_apply=%region_16.17 | all-reduce | flops 2 | bytes 16 | tf_op jit(solution)/shard_map/psum | solution.py:19
  221.4 2.3 multiply_subtract_fusion.28
  223.7 2.4 maximum_minimum_fusion.1
  228.7 2.2 multiply_reduce_fusion.1
  231.0 1.5 collective-permute-done.9
  233.2 3.0 collective-permute-start.11
  236.2 2.0 collective-permute-start.10
  241.7 7.1 %all-to-all-start.3 = ((f32[16,1,2,32,128]{4,3,2,1,0:T(8,128)}), f32[16,1,2,32,128]{4,3,2,1,0:T(8,128)}, u32[]{:S(2)}, u32[]{:S(2)}) async-start(f32[16,1,2,32,128]{4,3,2,1,0:T(8,128)} %broadcast_in_dim.122), calls=%async_computation.3 | async-start | bytes 1048576 | tf_op jit(solution)/shard_map/all_to_all | solution.py:31
  250.5 1.5 fusion.6
  252.0 2.5 fusion.9
  254.5 1.5 multiply_subtract_fusion.6
  256.5 1.8 multiply_subtract_fusion.1
  260.8 2.2 fusion.17
  266.6 3.8 %multiply_reduce_fusion.7 = (f32[]{:T(128)}, f32[64,32,128]{2,1,0:T(8,128)}) fusion(f32[2,64,32,128]{3,2,1,0:T(8,128)} %fusion.17, f32[64,32,128]{2,1,0:T(8,128)} %get-tuple-element.137), kind=kOutput, calls=%fused_computation.186 | convolution fusion | flops 403718144 | bytes 3145732 | tf_op jit(solution)/shard_map/xyj,jk->xyk/dot_general | solution.py:86
  270.5 1.4 copy.134
  276.5 2.5 multiply_reduce_fusion.6
  279.0 9.4 %all-reduce.12 = (f32[]{:T(128)}, f32[]{:T(128)}, f32[]{:T(128)}, f32[]{:T(128)}, f32[]{:T(128)}) all-reduce(f32[]{:T(128)} %get-tuple-element.132, f32[]{:T(128)} %multiply_reduce_fusion.6, f32[]{:T(128)S(6)} %div.35, f32[]{:T(128)S(6)} %div.34, f32[]{:T(128)S(6)} %div.33), channel_id=1, replica_groups=mesh['gx_0'=4,'gx_1'=4,'gy_0'=4,'gy_1'=2] {'gx_0'}, use_global_device_ids=true, to_apply=%region_24.25 | all-reduce | flops 5 | bytes 40 | tf_op jit(solution)/shard_map/psum | solution.py:19
  288.4 9.1 %all-reduce.9 = (f32[]{:T(128)}, f32[]{:T(128)}, f32[]{:T(128)}, f32[]{:T(128)}, f32[]{:T(128)}) all-reduce(f32[]{:T(128)} %get-tuple-element.21, f32[]{:T(128)} %get-tuple-element.22, f32[]{:T(128)} %get-tuple-element.23, f32[]{:T(128)} %get-tuple-element.24, ...), channel_id=1, replica_groups=mesh['gx_0'=4,'gx_1'=4,'gy_0'=4,'gy_1'=2] {'gx_1'}, use_global_device_ids=true, to_apply=%region_25.26 | all-reduce | flops 5 | bytes 40 | tf_op jit(solution)/shard_map/psum | solution.py:19
  297.4 7.4 %all-reduce.6 = (f32[]{:T(128)}, f32[]{:T(128)}, f32[]{:T(128)}, f32[]{:T(128)}, f32[]{:T(128)}) all-reduce(f32[]{:T(128)} %get-tuple-element.12, f32[]{:T(128)} %get-tuple-element.13, f32[]{:T(128)} %get-tuple-element.14, f32[]{:T(128)} %get-tuple-element.15, ...), channel_id=1, replica_groups=mesh['gx_0'=4,'gx_1'=4,'gy_0'=4,'gy_1'=2] {'gy_0'}, use_global_device_ids=true, to_apply=%region_26.27 | all-reduce | flops 5 | bytes 40 | tf_op jit(solution)/shard_map/psum | solution.py:19
  304.9 10.5 %all-reduce.15 = (f32[]{:T(128)}, f32[]{:T(128)}, f32[1]{0:T(128)}, f32[1]{0:T(128)}, f32[1]{0:T(128)}) all-reduce(f32[]{:T(128)} %get-tuple-element.3, f32[]{:T(128)} %get-tuple-element.4, f32[1]{0:T(128)} %bitcast.79, f32[1]{0:T(128)} %bitcast.75, f32[1]{0:T(128)} %bitcast.71), channel_id=1, replica_groups=mesh['gx_0'=4,'gx_1'=4,'gy_0'=4,'gy_1'=2] {'gy_1'}, use_global_device_ids=true, to_apply=%region_27.28 | all-reduce | flops 5 | bytes 40 | tf_op jit(solution)/shard_map/psum | solution.py:19
  316.8 3.1 multiply_subtract_fusion.27
  319.9 1.5 maximum_minimum_fusion
  321.3 2.5 pad_maximum_fusion.48
  (144 shorter events, 47.9 us)
Async XLA Ops:
  0.6 6.3 %copy-start = (f32[64,32,128]{2,1,0:T(8,128)S(1)}, f32[64,32,128]{2,1,0:T(8,128)}, u32[]{:S(2)}) copy-start(f32[64,32,128]{2,1,0:T(8,128)} %param.8) | copy-start | bytes 3145732
  0.6 18.1 %copy-start.1 = (f32[64,32,128]{2,1,0:T(8,128)S(1)}, f32[64,32,128]{2,1,0:T(8,128)}, u32[]{:S(2)}) copy-start(f32[64,32,128]{2,1,0:T(8,128)} %param.7) | copy-start | bytes 3145732
  0.7 18.1 %copy-start.6 = (f32[64,32,128]{2,1,0:T(8,128)S(1)}, f32[64,32,128]{2,1,0:T(8,128)}, u32[]{:S(2)}) copy-start(f32[64,32,128]{2,1,0:T(8,128)} %param.9) | copy-start | bytes 3145732
  1.6 22.7 %collective-permute-start = (f32[2,2,32,128]{3,2,1,0:T(8,128)S(1)}, f32[2,2,32,128]{3,2,1,0:T(8,128)S(1)}, u32[]{:S(2)}, u32[]{:S(2)}) collective-permute-start(f32[2,2,32,128]{3,2,1,0:T(8,128)S(1)} %get-tuple-element.91), channel_id=1, source_target_pairs={{0,8},{8,16},{16,24},{24,32},{32,40},{40,48},{48,56},{56,64},{64,7... | collective-permute-start | bytes 196616 | tf_op jit(solution)/shard_map/ppermute | solution.py:45
  5.6 18.8 %collective-permute-start.1 = (f32[2,2,32,128]{3,2,1,0:T(8,128)S(1)}, f32[2,2,32,128]{3,2,1,0:T(8,128)S(1)}, u32[]{:S(2)}, u32[]{:S(2)}) collective-permute-start(f32[2,2,32,128]{3,2,1,0:T(8,128)S(1)} %get-tuple-element.92), channel_id=1, source_target_pairs={{8,0},{16,8},{24,16},{32,24},{40,32},{48,40},{56,48},{64,56},{72,6... | collective-permute-start | bytes 196616 | tf_op jit(solution)/shard_map/ppermute | solution.py:46
  8.2 1.0 copy-start.19
  10.1 45.5 %all-to-all-start = ((f32[16,1,2,32,128]{4,3,2,1,0:T(8,128)}), f32[16,1,2,32,128]{4,3,2,1,0:T(8,128)}, u32[]{:S(2)}, u32[]{:S(2)}) async-start(f32[16,1,2,32,128]{4,3,2,1,0:T(8,128)} %broadcast_in_dim.119), calls=%async_computation | async-start | bytes 1048576 | tf_op jit(solution)/shard_map/all_to_all | solution.py:31
  18.7 3.4 %copy-start.27 = (s32[64,32,128]{2,1,0:T(8,128)S(1)}, s32[64,32,128]{2,1,0:T(8,128)}, u32[]{:S(2)}) copy-start(s32[64,32,128]{2,1,0:T(8,128)} %param.11) | copy-start | bytes 3145732
  22.1 9.1 %copy-start.29 = (f32[8]{0:T(128)S(1)}, f32[8]{0:T(128)}, u32[]{:S(2)}) copy-start(f32[8]{0:T(128)} %param.12) | copy-start | bytes 100
  22.1 9.8 %copy-start.30 = (f32[8]{0:T(128)S(1)}, f32[8]{0:T(128)}, u32[]{:S(2)}) copy-start(f32[8]{0:T(128)} %param.13) | copy-start | bytes 100
  24.5 8.1 %collective-permute-start.3 = (f32[2,68,2,128]{3,2,1,0:T(2,128)S(1)}, f32[2,68,2,128]{3,2,1,0:T(2,128)S(1)}, u32[]{:S(2)}, u32[]{:S(2)}) collective-permute-start(f32[2,68,2,128]{3,2,1,0:T(2,128)S(1)} %get-tuple-element.85), channel_id=1, source_target_pairs={{0,1},{1,2},{2,3},{3,4},{4,5},{5,6},{6,7},{8,9},{9,10},{10,11},{11... | collective-permute-start | bytes 417800 | tf_op jit(solution)/shard_map/ppermute | solution.py:45
  29.1 6.4 %collective-permute-start.2 = (f32[2,68,2,128]{3,2,1,0:T(2,128)S(1)}, f32[2,68,2,128]{3,2,1,0:T(2,128)S(1)}, u32[]{:S(2)}, u32[]{:S(2)}) collective-permute-start(f32[2,68,2,128]{3,2,1,0:T(2,128)S(1)} %get-tuple-element.86), channel_id=1, source_target_pairs={{1,0},{2,1},{3,2},{4,3},{5,4},{6,5},{7,6},{9,8},{10,9},{11,10},{12... | collective-permute-start | bytes 417800 | tf_op jit(solution)/shard_map/ppermute | solution.py:46
  43.2 1.3 copy-start.14
  43.2 1.7 copy-start.17
  47.8 3.7 %copy-start.24 = (f32[64,32,128]{2,0,1:T(8,128)S(1)}, f32[64,32,128]{2,0,1:T(8,128)}, u32[]{:S(2)}) copy-start(f32[64,32,128]{2,0,1:T(8,128)} %get-tuple-element.141) | copy-start | bytes 3145732
  57.0 0.8 copy-start.26
  57.8 20.7 %copy-start.3 = (f32[2,64,32,128]{3,2,1,0:T(8,128)S(1)}, f32[2,64,32,128]{3,2,1,0:T(8,128)}, u32[]{:S(2)}) copy-start(f32[2,64,32,128]{3,2,1,0:T(8,128)} %fusion.23) | copy-start | bytes 6291460
  62.5 14.7 %all-to-all-start.1 = ((f32[16,1,32,128]{3,2,1,0:T(8,128)}), f32[16,1,32,128]{3,2,1,0:T(8,128)}, u32[]{:S(2)}, u32[]{:S(2)}) async-start(f32[16,1,32,128]{3,2,1,0:T(8,128)} %broadcast_in_dim.120), calls=%async_computation.1 | async-start | bytes 524288 | tf_op jit(solution)/shard_map/all_to_all | solution.py:31
  78.5 40.1 %copy-start.28 = (pred[64,32,128]{2,1,0:T(8,128)(4,1)S(1)}, pred[64,32,128]{2,1,0:T(8,128)(4,1)}, u32[]{:S(2)}) copy-start(pred[64,32,128]{2,1,0:T(8,128)(4,1)} %get-tuple-element.93) | copy-start | bytes 786436
  133.3 2.9 copy-start.7
  133.3 5.1 %collective-permute-start.4 = (f32[2,2,32,128]{3,2,1,0:T(8,128)S(1)}, f32[2,2,32,128]{3,2,1,0:T(8,128)S(1)}, u32[]{:S(2)}, u32[]{:S(2)}) collective-permute-start(f32[2,2,32,128]{3,2,1,0:T(8,128)S(1)} %get-tuple-element.89), channel_id=1, source_target_pairs={{0,8},{8,16},{16,24},{24,32},{32,40},{40,48},{48,56},{56,64},{64,7... | collective-permute-start | bytes 196616 | tf_op jit(solution)/shard_map/ppermute | solution.py:45
  134.9 5.0 %collective-permute-start.5 = (f32[2,2,32,128]{3,2,1,0:T(8,128)S(1)}, f32[2,2,32,128]{3,2,1,0:T(8,128)S(1)}, u32[]{:S(2)}, u32[]{:S(2)}) collective-permute-start(f32[2,2,32,128]{3,2,1,0:T(8,128)S(1)} %get-tuple-element.90), channel_id=1, source_target_pairs={{8,0},{16,8},{24,16},{32,24},{40,32},{48,40},{56,48},{64,56},{72,6... | collective-permute-start | bytes 196616 | tf_op jit(solution)/shard_map/ppermute | solution.py:46
  140.0 16.1 %collective-permute-start.7 = (f32[2,68,2,128]{3,2,1,0:T(2,128)S(1)}, f32[2,68,2,128]{3,2,1,0:T(2,128)S(1)}, u32[]{:S(2)}, u32[]{:S(2)}) collective-permute-start(f32[2,68,2,128]{3,2,1,0:T(2,128)S(1)} %get-tuple-element.83), channel_id=1, source_target_pairs={{0,1},{1,2},{2,3},{3,4},{4,5},{5,6},{6,7},{8,9},{9,10},{10,11},{11... | collective-permute-start | bytes 417800 | tf_op jit(solution)/shard_map/ppermute | solution.py:45
  143.9 12.2 %collective-permute-start.6 = (f32[2,68,2,128]{3,2,1,0:T(2,128)S(1)}, f32[2,68,2,128]{3,2,1,0:T(2,128)S(1)}, u32[]{:S(2)}, u32[]{:S(2)}) collective-permute-start(f32[2,68,2,128]{3,2,1,0:T(2,128)S(1)} %get-tuple-element.84), channel_id=1, source_target_pairs={{1,0},{2,1},{3,2},{4,3},{5,4},{6,5},{7,6},{9,8},{10,9},{11,10},{12... | collective-permute-start | bytes 417800 | tf_op jit(solution)/shard_map/ppermute | solution.py:46
  147.2 1.0 copy-start.22
  149.1 28.7 %all-to-all-start.2 = ((f32[16,1,2,32,128]{4,3,2,1,0:T(8,128)}), f32[16,1,2,32,128]{4,3,2,1,0:T(8,128)}, u32[]{:S(2)}, u32[]{:S(2)}) async-start(f32[16,1,2,32,128]{4,3,2,1,0:T(8,128)} %broadcast_in_dim.121), calls=%async_computation.2 | async-start | bytes 1048576 | tf_op jit(solution)/shard_map/all_to_all | solution.py:31
  161.6 1.1 copy-start.2
  164.5 1.3 copy-start.15
  164.5 1.7 copy-start.18
  174.0 6.0 %copy-start.9 = (f32[64,32,128]{2,1,0:T(8,128)S(1)}, f32[64,32,128]{2,1,0:T(8,128)}, u32[]{:S(2)}) copy-start(f32[64,32,128]{2,1,0:T(8,128)} %param.10) | copy-start | bytes 3145732
  177.8 2.2 copy-start.23
  180.0 2.7 copy-start.4
  182.6 1.3 copy-start.5
  223.6 5.1 %copy-start.8 = (f32[64,32,128]{2,1,0:T(8,128)S(1)}, f32[64,32,128]{2,1,0:T(8,128)}, u32[]{:S(2)}) copy-start(f32[64,32,128]{2,1,0:T(8,128)} %param.9) | copy-start | bytes 3145732
  226.1 4.8 %collective-permute-start.8 = (f32[2,2,32,128]{3,2,1,0:T(8,128)S(1)}, f32[2,2,32,128]{3,2,1,0:T(8,128)S(1)}, u32[]{:S(2)}, u32[]{:S(2)}) collective-permute-start(f32[2,2,32,128]{3,2,1,0:T(8,128)S(1)} %get-tuple-element.87), channel_id=1, source_target_pairs={{0,8},{8,16},{16,24},{24,32},{32,40},{40,48},{48,56},{56,64},{64,7... | collective-permute-start | bytes 196616 | tf_op jit(solution)/shard_map/ppermute | solution.py:45
  227.4 5.0 %collective-permute-start.9 = (f32[2,2,32,128]{3,2,1,0:T(8,128)S(1)}, f32[2,2,32,128]{3,2,1,0:T(8,128)S(1)}, u32[]{:S(2)}, u32[]{:S(2)}) collective-permute-start(f32[2,2,32,128]{3,2,1,0:T(8,128)S(1)} %get-tuple-element.88), channel_id=1, source_target_pairs={{8,0},{16,8},{24,16},{32,24},{40,32},{48,40},{56,48},{64,56},{72,6... | collective-permute-start | bytes 196616 | tf_op jit(solution)/shard_map/ppermute | solution.py:46
  233.2 15.6 %collective-permute-start.11 = (f32[2,68,2,128]{3,2,1,0:T(2,128)}, f32[2,68,2,128]{3,2,1,0:T(2,128)S(1)}, u32[]{:S(2)}, u32[]{:S(2)}) collective-permute-start(f32[2,68,2,128]{3,2,1,0:T(2,128)} %get-tuple-element.81), channel_id=1, source_target_pairs={{0,1},{1,2},{2,3},{3,4},{4,5},{5,6},{6,7},{8,9},{9,10},{10,11},{11... | collective-permute-start | bytes 417800 | tf_op jit(solution)/shard_map/ppermute | solution.py:45
  236.2 12.6 %collective-permute-start.10 = (f32[2,68,2,128]{3,2,1,0:T(2,128)}, f32[2,68,2,128]{3,2,1,0:T(2,128)}, u32[]{:S(2)}, u32[]{:S(2)}) collective-permute-start(f32[2,68,2,128]{3,2,1,0:T(2,128)} %get-tuple-element.82), channel_id=1, source_target_pairs={{1,0},{2,1},{3,2},{4,3},{5,4},{6,5},{7,6},{9,8},{10,9},{11,10},{12... | collective-permute-start | bytes 417800 | tf_op jit(solution)/shard_map/ppermute | solution.py:46
  239.5 10.6 %copy-start.20 = (f32[64,32,128]{2,0,1:T(8,128)}, f32[64,32,128]{2,0,1:T(8,128)S(1)}, u32[]{:S(2)}) copy-start(f32[64,32,128]{2,0,1:T(8,128)S(1)} %get-tuple-element.135) | copy-start | bytes 3145732
  241.7 28.8 %all-to-all-start.3 = ((f32[16,1,2,32,128]{4,3,2,1,0:T(8,128)}), f32[16,1,2,32,128]{4,3,2,1,0:T(8,128)}, u32[]{:S(2)}, u32[]{:S(2)}) async-start(f32[16,1,2,32,128]{4,3,2,1,0:T(8,128)} %broadcast_in_dim.122), calls=%async_computation.3 | async-start | bytes 1048576 | tf_op jit(solution)/shard_map/all_to_all | solution.py:31
  258.3 1.3 copy-start.13
  258.3 1.7 copy-start.16
  266.6 6.0 %copy-start.10 = (f32[64,32,128]{2,1,0:T(8,128)S(1)}, f32[64,32,128]{2,1,0:T(8,128)}, u32[]{:S(2)}) copy-start(f32[64,32,128]{2,1,0:T(8,128)} %param.10) | copy-start | bytes 3145732
  270.5 2.2 copy-start.21
  316.8 3.1 copy-start.11
  316.8 3.1 copy-start.12
  316.8 3.1 copy-start.25
where the time goes:
time: 330 us; the launch traced here: 324 us
  blocking collectives  107 us (32%)
  other arithmetic  89.5 us (27%)
  starting transfers between devices  58 us (18%)
  matrix products  33.9 us (10%)
  between operations  14.7 us (4%)
  local copies, waits for them, and re-layouts  13.6 us (4%)
  waiting for transfers between devices  7.63 us (2%)
    psum x12, blocking collectives, over_axes(): value = lax.psum(value, axis)  107 us
    all_to_all x4, starting transfers between devices, copy_for_each(): return lax.all_to_all(copies, axis, split_axis=0, concat_axis=0, tiled=True)  29.8 us
    dot_general x6, matrix products, depth_prefix(): jnp.einsum('xyj,jk->xyk', values, table, precision=lax.Precision.HIGHEST)  19.6 us
    min x3, other arithmetic, local(): density_now = jnp.minimum(jnp.maximum(moved, lower_bound), upper_bound)  18.5 us
    ppermute x6, starting transfers between devices, with_halo(): before = lax.ppermute(last, axis, up)  18.4 us
    dot_general x6, matrix products, rows_prefix(): jnp.einsum('ij,jyz->iyz', table, values, precision=lax.Precision.HIGHEST)  9.99 us
    ppermute x6, starting transfers between devices, with_halo(): after = lax.ppermute(initial, axis, down)  9.84 us
    sub x3, other arithmetic, local(): slowness_now - ETA * grad_slowness * lax.rsqrt(norm_slowness / cells + EP...  7.55 us
  transfers between devices with their start and end apart: 16, of which 4 were waited for; matrix products, arithmetic and copies ran while one was open for 24% of the time, Pallas kernels for 0%

commit v1 on v0

--- a/solution.py
+++ b/solution.py
@@ -16,7 +16,7 @@
 
 def over_axes(value, axes):
     for axis in axes:
-        value = lax.psum(value, axis)
+        value = jnp.sum(lax.all_gather(value, axis), axis=0)
     return value
 
 

time: 330 us -> 396 us (1.20)
  local copies, waits for them, and re-layouts: 13.6 us -> 64.7 us
  other arithmetic: 89.5 us -> 113 us
  blocking collectives: 107 us -> 98.7 us
    psum x12 -> x0, blocking collectives: 107 us -> none  [over_axes(): value = lax.psum(value, axis)]
    unnamed x0 -> x12, blocking collectives: none -> 98.7 us
    unnamed x62 -> x146, local copies, waits for them, and re-layouts: 4.66 us -> 55.7 us
    reduce_sum x0 -> x36, other arithmetic: none -> 22.2 us  [over_axes(): value = jnp.sum(lax.all_gather(value, axis), axis=0)]
  transfers between devices with their start and end apart: 16 -> 16, of which waited for: 4 -> 4; matrix products, arithmetic and copies ran while one was open for 24% -> 20% of each run, Pallas kernels for 0% -> 0%
where the time goes in v1:
time: 396 us; the launch traced here: 389 us
  other arithmetic  113 us (29%)
  blocking collectives  98.7 us (25%)
  local copies, waits for them, and re-layouts  64.7 us (16%)
  starting transfers between devices  59 us (15%)
  matrix products  32.2 us (8%)
  between operations  15.6 us (4%)
  waiting for transfers between devices  6.3 us (2%)
    unnamed x12, blocking collectives  98.7 us
    unnamed x146, local copies, waits for them, and re-layouts  55.7 us
    all_to_all x4, starting transfers between devices, copy_for_each(): return lax.all_to_all(copies, axis, split_axis=0, concat_axis=0, tiled=True)  29.7 us
    reduce_sum x36, other arithmetic, over_axes(): value = jnp.sum(lax.all_gather(value, axis), axis=0)  22.2 us
    min x3, other arithmetic, local(): density_now = jnp.minimum(jnp.maximum(moved, lower_bound), upper_bound)  20.4 us
    ppermute x6, starting transfers between devices, with_halo(): before = lax.ppermute(last, axis, up)  19.3 us
    dot_general x6, matrix products, depth_prefix(): jnp.einsum('xyj,jk->xyk', values, table, precision=lax.Precision.HIGHEST)  17.9 us
    dot_general x6, matrix products, rows_prefix(): jnp.einsum('ij,jyz->iyz', table, values, precision=lax.Precision.HIGHEST)  9.98 us
  transfers between devices with their start and end apart: 16, of which 4 were waited for; matrix products, arithmetic and copies ran while one was open for 20% of the time, Pallas kernels for 0%

profile of v1, /device:TPU:1, one launch (start us, length us, event | category | flops | bytes accessed | tf_op | source)
XLA Modules:
  0.0 389.5 jit_solution(5007123911853393426)
XLA Ops:
  1.6 3.9 %collective-permute-start = (f32[2,2,32,128]{3,2,1,0:T(8,128)S(1)}, f32[2,2,32,128]{3,2,1,0:T(8,128)S(1)}, u32[]{:S(2)}, u32[]{:S(2)}) collective-permute-start(f32[2,2,32,128]{3,2,1,0:T(8,128)S(1)} %get-tuple-element.91), channel_id=1, source_target_pairs={{0,8},{8,16},{16,24},{24,32},{32,40},{40,48},{48,56},{56,64},{64,7... | collective-permute-start | bytes 196616 | tf_op jit(solution)/shard_map/ppermute | solution.py:45
  10.1 8.5 %all-to-all-start = ((f32[16,1,2,32,128]{4,3,2,1,0:T(8,128)}), f32[16,1,2,32,128]{4,3,2,1,0:T(8,128)}, u32[]{:S(2)}, u32[]{:S(2)}) async-start(f32[16,1,2,32,128]{4,3,2,1,0:T(8,128)} %broadcast_in_dim.119), calls=%async_computation | async-start | bytes 1048576 | tf_op jit(solution)/shard_map/all_to_all | solution.py:31
  18.7 3.4 multiply_reduce_fusion.5
  22.1 2.2 broadcast_compare_fusion
  24.5 4.6 %collective-permute-start.3 = (f32[2,68,2,128]{3,2,1,0:T(2,128)S(1)}, f32[2,68,2,128]{3,2,1,0:T(2,128)S(1)}, u32[]{:S(2)}, u32[]{:S(2)}) collective-permute-start(f32[2,68,2,128]{3,2,1,0:T(2,128)S(1)} %get-tuple-element.85), channel_id=1, source_target_pairs={{0,1},{1,2},{2,3},{3,4},{4,5},{5,6},{6,7},{8,9},{9,10},{10,11},{11... | collective-permute-start | bytes 417800 | tf_op jit(solution)/shard_map/ppermute | solution.py:45
  29.1 2.1 collective-permute-start.2
  36.3 1.5 fusion.2
  37.8 1.6 fusion.15
  39.4 1.5 multiply_subtract_fusion.24
  41.3 1.8 multiply_subtract_fusion.19
  45.6 2.2 fusion.23
  51.5 4.0 %multiply_reduce_fusion.11 = (f32[]{:T(128)}, f32[64,32,128]{2,1,0:T(8,128)}) fusion(f32[2,64,32,128]{3,2,1,0:T(8,128)} %fusion.23, f32[64,32,128]{2,0,1:T(8,128)S(1)} %copy-done.24), kind=kOutput, calls=%fused_computation.196 | convolution fusion | flops 403718144 | bytes 3145732 | tf_op jit(solution)/shard_map/xyj,jk->xyk/dot_general | solution.py:86
  59.0 4.0 %multiply_reduce_fusion.4 = (f32[]{:T(128)}, f32[64,32,128]{2,1,0:T(8,128)}, f32[32,128]{1,0:T(8,128)S(1)}) fusion(f32[64,32,128]{2,1,0:T(8,128)} %param.10, f32[32,128]{1,0:T(8,128)S(1)} %bitcast.279, f32[64,32,128]{2,0,1:T(8,128)} %copy-done.19), kind=kLoop, calls=%fused_computation.181 | loop fusion | flops 1568767 | bytes 3178500 | tf_op jit(solution)/shard_map/reduce_sum | solution.py:178
  63.7 7.3 %all-to-all-start.1 = ((f32[16,1,32,128]{3,2,1,0:T(8,128)}), f32[16,1,32,128]{3,2,1,0:T(8,128)}, u32[]{:S(2)}, u32[]{:S(2)}) async-start(f32[16,1,32,128]{3,2,1,0:T(8,128)} %broadcast_in_dim.120), calls=%async_computation.1 | async-start | bytes 524288 | tf_op jit(solution)/shard_map/all_to_all | solution.py:31
  71.1 3.4 fusion.59
  75.7 3.0 all-to-all-done.1
  80.0 2.6 multiply_reduce_fusion.10
  82.5 1.5 dynamic-update-slice.4
  85.2 6.6 %all-reduce.50 = (f32[4]{0:T(128)S(1)}, f32[4]{0:T(128)S(1)}) all-reduce(f32[4]{0:T(128)S(1)} %dynamic-update-slice, f32[4]{0:T(128)S(1)} %dynamic-update-slice.4), channel_id=1, replica_groups=mesh['gx_0'=4,'gx_1'=4,'gy_0'=4,'gy_1'=2] {'gx_0'}, use_global_device_ids=true, to_apply=%add.6 | all-reduce | flops 8 | bytes 64
  93.1 1.5 dynamic-update-slice.5
  96.0 7.5 %all-reduce.47 = (f32[4]{0:T(128)S(1)}, f32[4]{0:T(128)S(1)}) all-reduce(f32[4]{0:T(128)S(1)} %dynamic-update-slice.1, f32[4]{0:T(128)S(1)} %dynamic-update-slice.5), channel_id=1, replica_groups=mesh['gx_0'=4,'gx_1'=4,'gy_0'=4,'gy_1'=2] {'gx_1'}, use_global_device_ids=true, to_apply=%add.7 | all-reduce | flops 8 | bytes 64
  107.5 7.5 %all-reduce.44 = (f32[4]{0:T(128)S(1)}, f32[4]{0:T(128)S(1)}) all-reduce(f32[4]{0:T(128)S(1)} %dynamic-update-slice.2, f32[4]{0:T(128)S(1)} %dynamic-update-slice.6), channel_id=1, replica_groups=mesh['gx_0'=4,'gx_1'=4,'gy_0'=4,'gy_1'=2] {'gy_0'}, use_global_device_ids=true, to_apply=%add.8 | all-reduce | flops 8 | bytes 64
  119.6 10.2 %all-reduce.53 = (f32[2]{0:T(128)S(1)}, f32[2]{0:T(128)S(1)}) all-reduce(f32[2]{0:T(128)S(1)} %dynamic-update-slice.3, f32[2]{0:T(128)S(1)} %dynamic-update-slice.7), channel_id=1, replica_groups=mesh['gx_0'=4,'gx_1'=4,'gy_0'=4,'gy_1'=2] {'gy_1'}, use_global_device_ids=true, to_apply=%add.9 | all-reduce | flops 4 | bytes 32
  131.0 2.3 multiply_subtract_fusion.29
  134.6 14.7 %maximum_minimum_fusion.2 = (f32[64,32,128]{2,1,0:T(8,128)S(1)}, f32[64,32,128]{2,1,0:T(8,128)}, f32[64,32,128]{2,1,0:T(8,128)}) fusion(f32[64,32,128]{2,1,0:T(8,128)} %param.7, f32[64,32,128]{2,1,0:T(8,128)} %get-tuple-element.125, f32[]{:T(128)S(6)} %mul.590, pred[64,32,128]{2,1,0:T(8,128)(4,1)} %get-tuple-element.99, ...), kind=kLoop, calls=%fused_computation.194 | loop fusion | flops 5242880 | bytes 7340100 | tf_op jit(solution)/shard_map/min | solution.py:190
  149.3 2.8 collective-permute-start.4
  153.4 2.2 multiply_reduce_fusion.3
  155.6 1.5 collective-permute-done.5
  157.2 3.0 collective-permute-start.7
  160.2 2.0 collective-permute-start.6
  165.5 6.9 %all-to-all-start.2 = ((f32[16,1,2,32,128]{4,3,2,1,0:T(8,128)}), f32[16,1,2,32,128]{4,3,2,1,0:T(8,128)}, u32[]{:S(2)}, u32[]{:S(2)}) async-start(f32[16,1,2,32,128]{4,3,2,1,0:T(8,128)} %broadcast_in_dim.121), calls=%async_computation.2 | async-start | bytes 1048576 | tf_op jit(solution)/shard_map/all_to_all | solution.py:31
  173.3 1.5 fusion.4
  174.7 1.6 fusion.12
  177.4 1.8 multiply_subtract_fusion.10
  183.4 2.3 multiply_reduce_fusion.9
  194.7 2.6 fusion.36
  197.4 8.6 %all-reduce.49 = (f32[4]{0:T(128)S(1)}, f32[4]{0:T(128)S(1)}) all-reduce(f32[4]{0:T(128)S(1)} %dynamic-update-slice.8, f32[4]{0:T(128)S(1)} %dynamic-update-slice.12), channel_id=1, replica_groups=mesh['gx_0'=4,'gx_1'=4,'gy_0'=4,'gy_1'=2] {'gx_0'}, use_global_device_ids=true, to_apply=%add.14 | all-reduce | flops 8 | bytes 64
  206.6 1.6 dynamic-update-slice.13
  210.2 2.2 fusion.35
  212.4 8.4 %all-reduce.46 = (f32[4]{0:T(128)S(1)}, f32[4]{0:T(128)S(1)}) all-reduce(f32[4]{0:T(128)S(1)} %dynamic-update-slice.9, f32[4]{0:T(128)S(1)} %dynamic-update-slice.13), channel_id=1, replica_groups=mesh['gx_0'=4,'gx_1'=4,'gy_0'=4,'gy_1'=2] {'gx_1'}, use_global_device_ids=true, to_apply=%add.15 | all-reduce | flops 8 | bytes 64
  225.9 6.8 %all-reduce.43 = (f32[4]{0:T(128)S(1)}, f32[4]{0:T(128)S(1)}) all-reduce(f32[4]{0:T(128)S(1)} %dynamic-update-slice.10, f32[4]{0:T(128)S(1)} %dynamic-update-slice.14), channel_id=1, replica_groups=mesh['gx_0'=4,'gx_1'=4,'gy_0'=4,'gy_1'=2] {'gy_0'}, use_global_device_ids=true, to_apply=%add.16 | all-reduce | flops 8 | bytes 64
  237.2 9.8 %all-reduce.52 = (f32[2]{0:T(128)S(1)}, f32[2]{0:T(128)S(1)}) all-reduce(f32[2]{0:T(128)S(1)} %dynamic-update-slice.11, f32[2]{0:T(128)S(1)} %dynamic-update-slice.15), channel_id=1, replica_groups=mesh['gx_0'=4,'gx_1'=4,'gy_0'=4,'gy_1'=2] {'gy_1'}, use_global_device_ids=true, to_apply=%add.17 | all-reduce | flops 4 | bytes 32
  248.4 2.2 multiply_subtract_fusion.28
  251.9 2.4 maximum_minimum_fusion.1
  257.0 2.2 multiply_reduce_fusion.1
  259.2 1.5 collective-permute-done.9
  261.5 3.7 collective-permute-start.11
  265.3 1.9 collective-permute-start.10
  270.8 6.9 %all-to-all-start.3 = ((f32[16,1,2,32,128]{4,3,2,1,0:T(8,128)}), f32[16,1,2,32,128]{4,3,2,1,0:T(8,128)}, u32[]{:S(2)}, u32[]{:S(2)}) async-start(f32[16,1,2,32,128]{4,3,2,1,0:T(8,128)} %broadcast_in_dim.122), calls=%async_computation.3 | async-start | bytes 1048576 | tf_op jit(solution)/shard_map/all_to_all | solution.py:31
  280.2 1.5 fusion.6
  281.7 2.5 fusion.9
  284.2 1.5 multiply_subtract_fusion.6
  286.1 1.8 multiply_subtract_fusion.1
  290.4 2.2 fusion.17
  296.5 3.8 multiply_reduce_fusion.7
  308.5 2.5 multiply_reduce_fusion.6
  311.0 1.6 dynamic-update-slice.20
  312.6 8.5 %all-reduce.48 = (f32[4]{0:T(128)S(1)}, f32[4]{0:T(128)S(1)}, f32[4]{0:T(128)S(1)}, f32[4]{0:T(128)S(1)}, f32[4]{0:T(128)S(1)}) all-reduce(f32[4]{0:T(128)S(1)} %dynamic-update-slice.16, f32[4]{0:T(128)S(1)} %dynamic-update-slice.20, f32[4]{0:T(128)S(1)} %dynamic-update-slice.32, ...), channel_id=1, replica_groups=mesh['gx_0'=4,'gx_1'=4,'gy_0'=4,'gy_1'=2] {'gx_0'}, use_global_device_ids=true, to_apply=%add.22 | all-reduce | flops 20 | bytes 160
  331.3 8.4 %all-reduce.45 = (f32[4]{0:T(128)S(1)}, f32[4]{0:T(128)S(1)}, f32[4]{0:T(128)S(1)}, f32[4]{0:T(128)S(1)}, f32[4]{0:T(128)S(1)}) all-reduce(f32[4]{0:T(128)S(1)} %dynamic-update-slice.17, f32[4]{0:T(128)S(1)} %dynamic-update-slice.21, f32[4]{0:T(128)S(1)} %dynamic-update-slice.33, ...), channel_id=1, replica_groups=mesh['gx_0'=4,'gx_1'=4,'gy_0'=4,'gy_1'=2] {'gx_1'}, use_global_device_ids=true, to_apply=%add.23 | all-reduce | flops 20 | bytes 160
  349.3 6.7 %all-reduce.42 = (f32[4]{0:T(128)S(1)}, f32[4]{0:T(128)S(1)}, f32[4]{0:T(128)S(1)}, f32[4]{0:T(128)S(1)}, f32[4]{0:T(128)S(1)}) all-reduce(f32[4]{0:T(128)S(1)} %dynamic-update-slice.18, f32[4]{0:T(128)S(1)} %dynamic-update-slice.22, f32[4]{0:T(128)S(1)} %dynamic-update-slice.34, ...), channel_id=1, replica_groups=mesh['gx_0'=4,'gx_1'=4,'gy_0'=4,'gy_1'=2] {'gy_0'}, use_global_device_ids=true, to_apply=%add.24 | all-reduce | flops 20 | bytes 160
  365.9 9.8 %all-reduce.51 = (f32[2]{0:T(128)S(1)}, f32[2]{0:T(128)S(1)}, f32[2]{0:T(128)S(1)}, f32[2]{0:T(128)S(1)}, f32[2]{0:T(128)S(1)}) all-reduce(f32[2]{0:T(128)S(1)} %dynamic-update-slice.19, f32[2]{0:T(128)S(1)} %dynamic-update-slice.23, f32[2]{0:T(128)S(1)} %dynamic-update-slice.35, ...), channel_id=1, replica_groups=mesh['gx_0'=4,'gx_1'=4,'gy_0'=4,'gy_1'=2] {'gy_1'}, use_global_device_ids=true, to_apply=%add.25 | all-reduce | flops 10 | bytes 80
  377.0 2.9 multiply_subtract_fusion.27
  383.2 3.3 maximum_minimum_fusion
  386.5 2.5 pad_maximum_fusion.48
  (264 shorter events, 118.6 us)
Async XLA Ops:
  0.6 6.3 %copy-start = (f32[64,32,128]{2,1,0:T(8,128)S(1)}, f32[64,32,128]{2,1,0:T(8,128)}, u32[]{:S(2)}) copy-start(f32[64,32,128]{2,1,0:T(8,128)} %param.8) | copy-start | bytes 3145732
  0.6 18.1 %copy-start.1 = (f32[64,32,128]{2,1,0:T(8,128)S(1)}, f32[64,32,128]{2,1,0:T(8,128)}, u32[]{:S(2)}) copy-start(f32[64,32,128]{2,1,0:T(8,128)} %param.7) | copy-start | bytes 3145732
  0.7 18.1 %copy-start.9 = (f32[64,32,128]{2,1,0:T(8,128)S(1)}, f32[64,32,128]{2,1,0:T(8,128)}, u32[]{:S(2)}) copy-start(f32[64,32,128]{2,1,0:T(8,128)} %param.9) | copy-start | bytes 3145732
  1.6 22.7 %collective-permute-start = (f32[2,2,32,128]{3,2,1,0:T(8,128)S(1)}, f32[2,2,32,128]{3,2,1,0:T(8,128)S(1)}, u32[]{:S(2)}, u32[]{:S(2)}) collective-permute-start(f32[2,2,32,128]{3,2,1,0:T(8,128)S(1)} %get-tuple-element.91), channel_id=1, source_target_pairs={{0,8},{8,16},{16,24},{24,32},{32,40},{40,48},{48,56},{56,64},{64,7... | collective-permute-start | bytes 196616 | tf_op jit(solution)/shard_map/ppermute | solution.py:45
  5.6 18.8 %collective-permute-start.1 = (f32[2,2,32,128]{3,2,1,0:T(8,128)S(1)}, f32[2,2,32,128]{3,2,1,0:T(8,128)S(1)}, u32[]{:S(2)}, u32[]{:S(2)}) collective-permute-start(f32[2,2,32,128]{3,2,1,0:T(8,128)S(1)} %get-tuple-element.92), channel_id=1, source_target_pairs={{8,0},{16,8},{24,16},{32,24},{40,32},{48,40},{56,48},{64,56},{72,6... | collective-permute-start | bytes 196616 | tf_op jit(solution)/shard_map/ppermute | solution.py:46
  8.2 1.0 copy-start.19
  10.1 46.8 %all-to-all-start = ((f32[16,1,2,32,128]{4,3,2,1,0:T(8,128)}), f32[16,1,2,32,128]{4,3,2,1,0:T(8,128)}, u32[]{:S(2)}, u32[]{:S(2)}) async-start(f32[16,1,2,32,128]{4,3,2,1,0:T(8,128)} %broadcast_in_dim.119), calls=%async_computation | async-start | bytes 1048576 | tf_op jit(solution)/shard_map/all_to_all | solution.py:31
  18.7 3.4 copy-start.27
  22.1 9.2 %copy-start.29 = (f32[8]{0:T(128)S(1)}, f32[8]{0:T(128)}, u32[]{:S(2)}) copy-start(f32[8]{0:T(128)} %param.12) | copy-start | bytes 100
  22.1 9.9 %copy-start.34 = (u32[128]{0:T(128)S(1)}, u32[128]{0:T(128)}, u32[]{:S(2)}) copy-start(u32[128]{0:T(128)} %constant.110) | copy-start | bytes 1540
  22.1 10.5 %copy-start.33 = (u32[128]{0:T(128)S(1)}, u32[128]{0:T(128)}, u32[]{:S(2)}) copy-start(u32[128]{0:T(128)} %constant.105) | copy-start | bytes 1540
  22.1 11.1 %copy-start.32 = (u32[128]{0:T(128)S(1)}, u32[128]{0:T(128)}, u32[]{:S(2)}) copy-start(u32[128]{0:T(128)} %constant.100) | copy-start | bytes 1540
  22.1 11.7 %copy-start.31 = (u32[128]{0:T(128)S(1)}, u32[128]{0:T(128)}, u32[]{:S(2)}) copy-start(u32[128]{0:T(128)} %constant.95) | copy-start | bytes 1540
  22.1 12.3 %copy-start.30 = (f32[8]{0:T(128)S(1)}, f32[8]{0:T(128)}, u32[]{:S(2)}) copy-start(f32[8]{0:T(128)} %param.13) | copy-start | bytes 100
  24.5 10.6 %collective-permute-start.3 = (f32[2,68,2,128]{3,2,1,0:T(2,128)S(1)}, f32[2,68,2,128]{3,2,1,0:T(2,128)S(1)}, u32[]{:S(2)}, u32[]{:S(2)}) collective-permute-start(f32[2,68,2,128]{3,2,1,0:T(2,128)S(1)} %get-tuple-element.85), channel_id=1, source_target_pairs={{0,1},{1,2},{2,3},{3,4},{4,5},{5,6},{6,7},{8,9},{9,10},{10,11},{11... | collective-permute-start | bytes 417800 | tf_op jit(solution)/shard_map/ppermute | solution.py:45
  29.1 6.4 %collective-permute-start.2 = (f32[2,68,2,128]{3,2,1,0:T(2,128)S(1)}, f32[2,68,2,128]{3,2,1,0:T(2,128)S(1)}, u32[]{:S(2)}, u32[]{:S(2)}) collective-permute-start(f32[2,68,2,128]{3,2,1,0:T(2,128)S(1)} %get-tuple-element.86), channel_id=1, source_target_pairs={{1,0},{2,1},{3,2},{4,3},{5,4},{6,5},{7,6},{9,8},{10,9},{11,10},{12... | collective-permute-start | bytes 417800 | tf_op jit(solution)/shard_map/ppermute | solution.py:46
  43.1 1.3 copy-start.15
  43.1 1.7 copy-start.17
  47.8 3.7 copy-start.24
  58.2 0.8 copy-start.26
  59.0 20.9 %copy-start.4 = (f32[2,64,32,128]{3,2,1,0:T(8,128)S(1)}, f32[2,64,32,128]{3,2,1,0:T(8,128)}, u32[]{:S(2)}) copy-start(f32[2,64,32,128]{3,2,1,0:T(8,128)} %fusion.23) | copy-start | bytes 6291460
  63.7 14.9 %all-to-all-start.1 = ((f32[16,1,32,128]{3,2,1,0:T(8,128)}), f32[16,1,32,128]{3,2,1,0:T(8,128)}, u32[]{:S(2)}, u32[]{:S(2)}) async-start(f32[16,1,32,128]{3,2,1,0:T(8,128)} %broadcast_in_dim.120), calls=%async_computation.1 | async-start | bytes 524288 | tf_op jit(solution)/shard_map/all_to_all | solution.py:31
  82.5 52.1 %copy-start.28 = (pred[64,32,128]{2,1,0:T(8,128)(4,1)S(1)}, pred[64,32,128]{2,1,0:T(8,128)(4,1)}, u32[]{:S(2)}) copy-start(pred[64,32,128]{2,1,0:T(8,128)(4,1)} %get-tuple-element.93) | copy-start | bytes 786436
  149.3 4.1 %copy-start.10 = (f32[64,32,128]{2,1,0:T(8,128)S(1)}, f32[64,32,128]{2,1,0:T(8,128)}, u32[]{:S(2)}) copy-start(f32[64,32,128]{2,1,0:T(8,128)} %param.9) | copy-start | bytes 3145732
  149.3 6.3 %collective-permute-start.4 = (f32[2,2,32,128]{3,2,1,0:T(8,128)S(1)}, f32[2,2,32,128]{3,2,1,0:T(8,128)S(1)}, u32[]{:S(2)}, u32[]{:S(2)}) collective-permute-start(f32[2,2,32,128]{3,2,1,0:T(8,128)S(1)} %get-tuple-element.89), channel_id=1, source_target_pairs={{0,8},{8,16},{16,24},{24,32},{32,40},{40,48},{48,56},{56,64},{64,7... | collective-permute-start | bytes 196616 | tf_op jit(solution)/shard_map/ppermute | solution.py:45
  152.1 5.0 %collective-permute-start.5 = (f32[2,2,32,128]{3,2,1,0:T(8,128)S(1)}, f32[2,2,32,128]{3,2,1,0:T(8,128)S(1)}, u32[]{:S(2)}, u32[]{:S(2)}) collective-permute-start(f32[2,2,32,128]{3,2,1,0:T(8,128)S(1)} %get-tuple-element.90), channel_id=1, source_target_pairs={{8,0},{16,8},{24,16},{32,24},{40,32},{48,40},{56,48},{64,56},{72,6... | collective-permute-start | bytes 196616 | tf_op jit(solution)/shard_map/ppermute | solution.py:46
  157.2 15.2 %collective-permute-start.7 = (f32[2,68,2,128]{3,2,1,0:T(2,128)S(1)}, f32[2,68,2,128]{3,2,1,0:T(2,128)S(1)}, u32[]{:S(2)}, u32[]{:S(2)}) collective-permute-start(f32[2,68,2,128]{3,2,1,0:T(2,128)S(1)} %get-tuple-element.83), channel_id=1, source_target_pairs={{0,1},{1,2},{2,3},{3,4},{4,5},{5,6},{6,7},{8,9},{9,10},{10,11},{11... | collective-permute-start | bytes 417800 | tf_op jit(solution)/shard_map/ppermute | solution.py:45
  160.2 12.3 %collective-permute-start.6 = (f32[2,68,2,128]{3,2,1,0:T(2,128)S(1)}, f32[2,68,2,128]{3,2,1,0:T(2,128)S(1)}, u32[]{:S(2)}, u32[]{:S(2)}) collective-permute-start(f32[2,68,2,128]{3,2,1,0:T(2,128)S(1)} %get-tuple-element.84), channel_id=1, source_target_pairs={{1,0},{2,1},{3,2},{4,3},{5,4},{6,5},{7,6},{9,8},{10,9},{11,10},{12... | collective-permute-start | bytes 417800 | tf_op jit(solution)/shard_map/ppermute | solution.py:46
  163.5 1.0 copy-start.22
  165.5 21.6 %all-to-all-start.2 = ((f32[16,1,2,32,128]{4,3,2,1,0:T(8,128)}), f32[16,1,2,32,128]{4,3,2,1,0:T(8,128)}, u32[]{:S(2)}, u32[]{:S(2)}) async-start(f32[16,1,2,32,128]{4,3,2,1,0:T(8,128)} %broadcast_in_dim.121), calls=%async_computation.2 | async-start | bytes 1048576 | tf_op jit(solution)/shard_map/all_to_all | solution.py:31
  176.8 2.4 copy-start.2
  176.8 2.3 copy-start.3
  177.4 1.8 copy-start.7
  179.2 1.3 copy-start.18
  181.2 2.2 copy-start.25
  182.1 1.4 copy-start.5
  183.4 5.9 %copy-start.12 = (f32[64,32,128]{2,1,0:T(8,128)S(1)}, f32[64,32,128]{2,1,0:T(8,128)}, u32[]{:S(2)}) copy-start(f32[64,32,128]{2,1,0:T(8,128)} %param.10) | copy-start | bytes 3145732
  187.1 2.2 copy-start.23
  189.3 2.8 copy-start.6
  192.0 1.4 copy-start.8
  251.9 5.1 %copy-start.11 = (f32[64,32,128]{2,1,0:T(8,128)S(1)}, f32[64,32,128]{2,1,0:T(8,128)}, u32[]{:S(2)}) copy-start(f32[64,32,128]{2,1,0:T(8,128)} %param.9) | copy-start | bytes 3145732
  254.4 4.8 %collective-permute-start.8 = (f32[2,2,32,128]{3,2,1,0:T(8,128)S(1)}, f32[2,2,32,128]{3,2,1,0:T(8,128)S(1)}, u32[]{:S(2)}, u32[]{:S(2)}) collective-permute-start(f32[2,2,32,128]{3,2,1,0:T(8,128)S(1)} %get-tuple-element.87), channel_id=1, source_target_pairs={{0,8},{8,16},{16,24},{24,32},{32,40},{40,48},{48,56},{56,64},{64,7... | collective-permute-start | bytes 196616 | tf_op jit(solution)/shard_map/ppermute | solution.py:45
  255.7 5.0 %collective-permute-start.9 = (f32[2,2,32,128]{3,2,1,0:T(8,128)S(1)}, f32[2,2,32,128]{3,2,1,0:T(8,128)S(1)}, u32[]{:S(2)}, u32[]{:S(2)}) collective-permute-start(f32[2,2,32,128]{3,2,1,0:T(8,128)S(1)} %get-tuple-element.88), channel_id=1, source_target_pairs={{8,0},{16,8},{24,16},{32,24},{40,32},{48,40},{56,48},{64,56},{72,6... | collective-permute-start | bytes 196616 | tf_op jit(solution)/shard_map/ppermute | solution.py:46
  261.5 17.0 %collective-permute-start.11 = (f32[2,68,2,128]{3,2,1,0:T(2,128)}, f32[2,68,2,128]{3,2,1,0:T(2,128)S(1)}, u32[]{:S(2)}, u32[]{:S(2)}) collective-permute-start(f32[2,68,2,128]{3,2,1,0:T(2,128)} %get-tuple-element.81), channel_id=1, source_target_pairs={{0,1},{1,2},{2,3},{3,4},{4,5},{5,6},{6,7},{8,9},{9,10},{10,11},{11... | collective-permute-start | bytes 417800 | tf_op jit(solution)/shard_map/ppermute | solution.py:45
  265.3 13.3 %collective-permute-start.10 = (f32[2,68,2,128]{3,2,1,0:T(2,128)}, f32[2,68,2,128]{3,2,1,0:T(2,128)}, u32[]{:S(2)}, u32[]{:S(2)}) collective-permute-start(f32[2,68,2,128]{3,2,1,0:T(2,128)} %get-tuple-element.82), channel_id=1, source_target_pairs={{1,0},{2,1},{3,2},{4,3},{5,4},{6,5},{7,6},{9,8},{10,9},{11,10},{12... | collective-permute-start | bytes 417800 | tf_op jit(solution)/shard_map/ppermute | solution.py:46
  268.5 11.3 %copy-start.20 = (f32[64,32,128]{2,0,1:T(8,128)}, f32[64,32,128]{2,0,1:T(8,128)S(1)}, u32[]{:S(2)}) copy-start(f32[64,32,128]{2,0,1:T(8,128)S(1)} %get-tuple-element.135) | copy-start | bytes 3145732
  270.8 30.9 %all-to-all-start.3 = ((f32[16,1,2,32,128]{4,3,2,1,0:T(8,128)}), f32[16,1,2,32,128]{4,3,2,1,0:T(8,128)}, u32[]{:S(2)}, u32[]{:S(2)}) async-start(f32[16,1,2,32,128]{4,3,2,1,0:T(8,128)} %broadcast_in_dim.122), calls=%async_computation.3 | async-start | bytes 1048576 | tf_op jit(solution)/shard_map/all_to_all | solution.py:31
  287.9 1.3 copy-start.14
  287.9 1.7 copy-start.16
  296.5 7.4 %copy-start.13 = (f32[64,32,128]{2,1,0:T(8,128)S(1)}, f32[64,32,128]{2,1,0:T(8,128)}, u32[]{:S(2)}) copy-start(f32[64,32,128]{2,1,0:T(8,128)} %param.10) | copy-start | bytes 3145732
  301.7 2.2 copy-start.21
